TPU v7x, 32 devices: a whole 2x2x4 slice. The times are simulated.
32 devices in a mesh: rep: 8 (over z, y), shard: 4 (over x, core).
Axes of the slice: x: 2, y: 2, z: 4, core: 2. Of those that a mesh axis runs over, the one named last changes fastest.
Arguments:
- prompt: bfloat16 [8, 1024, 768], P('rep', 'shard'), may hold values from -6 to 6
- conts: bfloat16 [8, 4, 512, 768], P('rep', 'shard'), may hold values from -6 to 6
- prompt_cot: bfloat16 [8, 1024, 768], P('rep', 'shard'), may hold values from -6 to 6
- cont_cot: bfloat16 [8, 4, 512, 768], P('rep', 'shard'), may hold values from -6 to 6
- labels: int32 [8, 4], P('rep', 'shard'), may hold values from 0 to 13
- w_qkv: float32 [768, 2304], P('shard'), may hold values from -0.21875 to 0.21875
- w_out: float32 [768, 768], P('shard'), may hold values from -3.5 to 3.5
- w_in: float32 [768, 3072], P('shard'), may hold values from -0.21875 to 0.21875
- w_ffo: float32 [3072, 768], P('shard'), may hold values from -0.109375 to 0.109375
- layer_biases: float32 [6, 768], replicated, may hold values from -3 to 3
- norm_gains: float32 [2, 768], replicated, may hold values from 0.25 to 1.75
- bias_in: float32 [3072], replicated, may hold values from -3 to 3
- w_student: float32 [768, 128], replicated, may hold values from -0.21875 to 0.21875
- student_vectors: float32 [3, 128], replicated, may hold values from -4 to 4
- w_pool: float32 [128, 128], replicated, may hold values from -0.5 to 0.5
- w_class: float32 [128, 14], replicated, may hold values from -1 to 1
- bias_class: float32 [14], replicated, may hold values from -3 to 3
Outputs:
- prompt_out: bfloat16 [8, 1024, 768], P('rep', 'shard')
- cont_out: bfloat16 [8, 4, 512, 768], P('rep', 'shard')
- logits: float32 [8, 4, 14], P('rep', 'shard')
- prompt_grad: float32 [8, 1024, 768], P('rep', 'shard')
- cont_grad: float32 [8, 4, 512, 768], P('rep', 'shard')
- grad_qkv: float32 [768, 2304], P('shard')
- grad_out: float32 [768, 768], P('shard')
- grad_in: float32 [768, 3072], P('shard')
- grad_ffo: float32 [3072, 768], P('shard')
- grad_biases: float32 [6, 768], replicated
- grad_gains: float32 [2, 768], replicated
- grad_bias_in: float32 [3072], replicated
- grad_student: float32 [768, 128], replicated
- grad_student_vectors: float32 [3, 128], replicated
- grad_pool: float32 [128, 128], replicated
- grad_class: float32 [128, 14], replicated
- grad_bias_class: float32 [14], replicated
All inputs are finite; a program needn't handle non-finite values.
Results may differ from a plain program's by a relative error of at most 0.02.
Values may be sent and summed in bfloat16 or wider, within the bound.
A program may use at most 192 MiB of HBM per device.

v0:
```python
import jax
import jax.numpy as jnp
from jax import lax
from jax.sharding import PartitionSpec as P

D = 768
HEADS = 12
DH = 64
STU = 128
SHEADS = 2
HIGHEST = lax.Precision.HIGHEST
NEG_BIG = -1e30


def dot_plain(left, right):
    return jnp.dot(left, right, preferred_element_type=jnp.float32)


def dot_first(left, right):
    return lax.dot_general(
        left, right, (((0,), (0,)), ((), ())), preferred_element_type=jnp.float32
    )


def dot_second(left, right):
    return lax.dot_general(
        left, right, (((1,), (1,)), ((), ())), preferred_element_type=jnp.float32
    )


def column_slice(matrix, head_index):
    return lax.dynamic_slice_in_dim(matrix, head_index * DH, DH, 1)


def layer_norm(values, gain, shift):
    center = values - jnp.mean(values, -1, keepdims=True)
    spread = jnp.mean(center * center, -1, keepdims=True)
    return center * lax.rsqrt(spread + 1e-05) * gain + shift


def gelu_exact(values):
    return jax.nn.gelu(values, approximate=False)


def attend_forward(queries, keys_all, values_all, allowed):
    scaling = DH ** (-0.5)

    def one_head(head_index):
        scores = jnp.where(
            allowed,
            dot_second(column_slice(queries, head_index), column_slice(keys_all, head_index))
            * scaling,
            NEG_BIG,
        )
        largest = jnp.max(scores, 1, keepdims=True)
        expo = jnp.exp(scores - largest)
        total = jnp.sum(expo, 1, keepdims=True)
        probs = (expo / total).astype(jnp.bfloat16)
        return (
            dot_plain(probs, column_slice(values_all, head_index)),
            (largest + jnp.log(total))[:, 0],
        )

    heads, log_totals = lax.map(one_head, jnp.arange(HEADS))
    return (heads.transpose(1, 0, 2).reshape(queries.shape[0], HEADS * DH), log_totals)


def attend_backward(queries, keys_all, values_all, allowed, grad_att, log_totals):
    scaling = DH ** (-0.5)

    def one_head(item):
        head_index, log_row = item
        query_h = column_slice(queries, head_index)
        key_h = column_slice(keys_all, head_index)
        grad_h = column_slice(grad_att, head_index)
        scores = jnp.where(allowed, dot_second(query_h, key_h) * scaling, NEG_BIG)
        probs = jnp.exp(scores - log_row[:, None])
        grad_probs = dot_second(grad_h, column_slice(values_all, head_index))
        delta = jnp.sum(grad_probs * probs, 1, keepdims=True)
        grad_scores = (probs * (grad_probs - delta)).astype(jnp.bfloat16)
        grad_query = dot_plain(grad_scores, key_h) * scaling
        grad_key = dot_first(grad_scores, query_h) * scaling
        grad_value = dot_first(probs.astype(jnp.bfloat16), grad_h)
        return (grad_query, grad_key, grad_value)

    grad_q, grad_k, grad_v = lax.map(one_head, (jnp.arange(HEADS), log_totals))

    def merge_heads(block):
        return block.transpose(1, 0, 2).reshape(block.shape[1], HEADS * DH)

    return (merge_heads(grad_q), merge_heads(grad_k), merge_heads(grad_v))


def student_loss(stu_rows, pool_query, bias_pool, w_pool, w_class, bias_class, label_value):
    part_w = STU // SHEADS
    parts = stu_rows.reshape(stu_rows.shape[0], SHEADS, part_w)
    queries = pool_query.reshape(SHEADS, part_w)
    scores = jnp.einsum("tha,ha->ht", parts, queries, precision=HIGHEST) * part_w ** (-0.5)
    largest = jnp.max(scores, -1, keepdims=True)
    expo = jnp.exp(scores - largest)
    weights = expo / jnp.sum(expo, -1, keepdims=True)
    pooled = jnp.einsum("ht,tha->ha", weights, parts, precision=HIGHEST).reshape(STU)
    top_layer = jnp.tanh(jnp.dot(pooled, w_pool, precision=HIGHEST) + bias_pool)
    logit_row = jnp.dot(top_layer, w_class, precision=HIGHEST) + bias_class
    top_logit = jnp.max(logit_row)
    log_total = jnp.log(jnp.sum(jnp.exp(logit_row - top_logit))) + top_logit
    picked = jnp.sum(jnp.where(jnp.arange(logit_row.shape[0]) == label_value, logit_row, 0.0))
    return (log_total - picked, logit_row)


def body(
    prompt,
    conts,
    prompt_cot,
    cont_cot,
    labels,
    w_qkv,
    w_out,
    w_in,
    w_ffo,
    layer_biases,
    norm_gains,
    bias_in,
    w_student,
    student_vectors,
    w_pool,
    w_class,
    bias_class,
):
    prompt_rows = prompt.shape[1]
    cont_len = conts.shape[2]
    prompt_len = prompt_rows * lax.axis_size("shard")
    qkv_low = w_qkv.astype(jnp.bfloat16)
    out_low = w_out.astype(jnp.bfloat16)
    in_low = w_in.astype(jnp.bfloat16)
    ffo_low = w_ffo.astype(jnp.bfloat16)
    qkv_full, out_full, in_full, ffo_full = (
        lax.all_gather(qkv_low, "shard", axis=0, tiled=True),
        lax.all_gather(out_low, "shard", axis=0, tiled=True),
        lax.all_gather(in_low, "shard", axis=0, tiled=True),
        lax.all_gather(ffo_low, "shard", axis=0, tiled=True),
    )
    tokens = jnp.concatenate([prompt[0], conts[0, 0]], 0)
    tokens_f = tokens.astype(jnp.float32)
    zero_row = jnp.zeros((D,), jnp.float32)
    bias_three = jnp.concatenate([layer_biases[0], zero_row, layer_biases[1]])
    qkv_b = (dot_plain(tokens, qkv_full) + bias_three).astype(jnp.bfloat16)
    queries = qkv_b[:, :D]
    keys_own = qkv_b[:, D : 2 * D]
    values_own = qkv_b[:, 2 * D :]
    prompt_keys, prompt_values = (
        lax.all_gather(keys_own[:prompt_rows], "shard", axis=0, tiled=True),
        lax.all_gather(values_own[:prompt_rows], "shard", axis=0, tiled=True),
    )
    keys_all = jnp.concatenate([prompt_keys, keys_own[prompt_rows:]], 0)
    values_all = jnp.concatenate([prompt_values, values_own[prompt_rows:]], 0)
    key_pos = jnp.arange(prompt_len + cont_len)
    query_pos = jnp.concatenate(
        [
            lax.axis_index("shard") * prompt_rows + jnp.arange(prompt_rows),
            prompt_len + jnp.arange(cont_len),
        ]
    )
    allowed = key_pos[None, :] <= query_pos[:, None]
    attended, log_totals = attend_forward(queries, keys_all, values_all, allowed)
    att_b = attended.astype(jnp.bfloat16)
    branch = dot_plain(att_b, out_full) + layer_biases[2]
    resid_one = tokens_f + branch
    first = layer_norm(resid_one, norm_gains[0], layer_biases[4])
    first_b = first.astype(jnp.bfloat16)
    hidden = dot_plain(first_b, in_full) + bias_in
    act_b = gelu_exact(hidden).astype(jnp.bfloat16)
    ffn = dot_plain(act_b, ffo_full) + layer_biases[3]
    resid_two = first + ffn
    output = layer_norm(resid_two, norm_gains[1], layer_biases[5])
    output_b = output.astype(jnp.bfloat16)
    cont_b = output_b[prompt_rows:]
    student_low = w_student.astype(jnp.bfloat16)
    stu = dot_plain(cont_b, student_low) + student_vectors[0]

    def loss_closed(stu_rows, pool_query, bias_pool, pool_weight, class_weight, class_bias):
        return student_loss(
            stu_rows, pool_query, bias_pool, pool_weight, class_weight, class_bias, labels[0, 0]
        )

    loss_value, loss_pull, logit_row = jax.vjp(
        loss_closed,
        stu,
        student_vectors[1],
        student_vectors[2],
        w_pool,
        w_class,
        bias_class,
        has_aux=True,
    )
    g_stu, g_query, g_pbias, g_pool, g_class, g_cbias = loss_pull(jnp.ones((), jnp.float32))
    g_stu_b = g_stu.astype(jnp.bfloat16)
    g_sbias = jnp.sum(g_stu_b.astype(jnp.float32), 0)
    g_student = dot_first(cont_b, g_stu_b)
    student_back = dot_second(g_stu_b, student_low)
    g_output = jnp.concatenate([prompt_cot[0], cont_cot[0, 0]], 0).astype(jnp.float32)
    g_output = g_output + jnp.concatenate(
        [jnp.zeros((prompt_rows, D), jnp.float32), student_back], 0
    )
    qkv_back, out_back, in_back, ffo_back = (
        lax.all_gather(qkv_low, "shard", axis=0, tiled=True),
        lax.all_gather(out_low, "shard", axis=0, tiled=True),
        lax.all_gather(in_low, "shard", axis=0, tiled=True),
        lax.all_gather(ffo_low, "shard", axis=0, tiled=True),
    )
    norm_two, norm_two_pull = jax.vjp(layer_norm, resid_two, norm_gains[1], layer_biases[5])
    g_resid_two, g_gain_two, g_shift_two = norm_two_pull(g_output)
    g_ffn_b = g_resid_two.astype(jnp.bfloat16)
    g_ffo = dot_first(act_b, g_ffn_b)
    g_ffo_bias = jnp.sum(g_ffn_b.astype(jnp.float32), 0)
    g_act = dot_second(g_ffn_b, ffo_back)
    gelu_value, gelu_pull = jax.vjp(gelu_exact, hidden)
    g_hidden_b = gelu_pull(g_act)[0].astype(jnp.bfloat16)
    g_in = dot_first(first_b, g_hidden_b)
    g_in_bias = jnp.sum(g_hidden_b.astype(jnp.float32), 0)
    g_first = g_resid_two + dot_second(g_hidden_b, in_back)
    norm_one, norm_one_pull = jax.vjp(layer_norm, resid_one, norm_gains[0], layer_biases[4])
    g_resid_one, g_gain_one, g_shift_one = norm_one_pull(g_first)
    g_branch_b = g_resid_one.astype(jnp.bfloat16)
    g_outw = dot_first(att_b, g_branch_b)
    g_out_bias = jnp.sum(g_branch_b.astype(jnp.float32), 0)
    g_att_b = dot_second(g_branch_b, out_back).astype(jnp.bfloat16)
    g_query_rows, g_keys_all, g_values_all = attend_backward(
        queries, keys_all, values_all, allowed, g_att_b, log_totals
    )
    query_grad_b = g_query_rows.astype(jnp.bfloat16)
    cont_kv_b = jnp.concatenate([g_keys_all[prompt_len:], g_values_all[prompt_len:]], 1).astype(
        jnp.bfloat16
    )
    block_kv_b = jnp.concatenate([g_keys_all[:prompt_len], g_values_all[:prompt_len]], 1).astype(
        jnp.bfloat16
    )
    kv_weights = qkv_back[:, D:]
    g_query_w = dot_first(tokens, query_grad_b)
    g_kv_w = dot_first(tokens[prompt_rows:], cont_kv_b)
    g_tokens = g_resid_one + dot_second(query_grad_b, qkv_back[:, :D])
    cont_through = dot_second(cont_kv_b, kv_weights)
    kv_summed = lax.psum_scatter(
        block_kv_b.astype(jnp.float32).astype(jnp.bfloat16),
        "shard",
        scatter_dimension=0,
        tiled=True,
    ).astype(jnp.float32)
    g_kv_w = g_kv_w + lax.dot_general(
        tokens_f[:prompt_rows],
        kv_summed,
        (((0,), (0,)), ((), ())),
        precision=HIGHEST,
        preferred_element_type=jnp.float32,
    )
    prompt_through = jnp.dot(
        kv_summed,
        kv_weights.astype(jnp.float32).T,
        precision=HIGHEST,
        preferred_element_type=jnp.float32,
    )
    value_cols = jnp.sum(kv_summed[:, D:], 0)
    g_tokens = g_tokens + jnp.concatenate([prompt_through, cont_through], 0)
    g_qkvw = jnp.concatenate([g_query_w, g_kv_w], 1)
    g_query_bias = jnp.sum(query_grad_b.astype(jnp.float32), 0)
    g_value_bias = jnp.sum(cont_kv_b[:, D:].astype(jnp.float32), 0) + value_cols
    owned = (
        lax.psum_scatter(
            g_qkvw.astype(jnp.bfloat16), "shard", scatter_dimension=0, tiled=True
        ).astype(jnp.float32),
        lax.psum_scatter(
            g_outw.astype(jnp.bfloat16), "shard", scatter_dimension=0, tiled=True
        ).astype(jnp.float32),
        lax.psum_scatter(
            g_in.astype(jnp.bfloat16), "shard", scatter_dimension=0, tiled=True
        ).astype(jnp.float32),
        lax.psum_scatter(
            g_ffo.astype(jnp.bfloat16), "shard", scatter_dimension=0, tiled=True
        ).astype(jnp.float32),
    )
    owned_qkv, owned_out, owned_in, owned_ffo = (
        lax.psum(owned[0].astype(jnp.bfloat16), "rep").astype(jnp.float32),
        lax.psum(owned[1].astype(jnp.bfloat16), "rep").astype(jnp.float32),
        lax.psum(owned[2].astype(jnp.bfloat16), "rep").astype(jnp.float32),
        lax.psum(owned[3].astype(jnp.bfloat16), "rep").astype(jnp.float32),
    )
    g_biases = jnp.stack(
        [g_query_bias, g_value_bias, g_out_bias, g_ffo_bias, g_shift_one, g_shift_two]
    )
    g_gains = jnp.stack([g_gain_one, g_gain_two])
    g_vectors = jnp.stack([g_sbias, g_query, g_pbias])
    summed = lax.psum(
        (g_biases, g_gains, g_in_bias, g_student, g_vectors, g_pool, g_class, g_cbias),
        ("rep", "shard"),
    )
    return (
        output_b[:prompt_rows][None],
        output_b[prompt_rows:][None, None],
        logit_row[None, None],
        g_tokens[:prompt_rows][None],
        g_tokens[prompt_rows:][None, None],
        owned_qkv,
        owned_out,
        owned_in,
        owned_ffo,
        summed[0],
        summed[1],
        summed[2],
        summed[3],
        summed[4],
        summed[5],
        summed[6],
        summed[7],
    )


def solution(mesh):
    return jax.shard_map(
        body,
        mesh=mesh,
        in_specs=(
            P("rep", "shard", None),
            P("rep", "shard", None, None),
            P("rep", "shard", None),
            P("rep", "shard", None, None),
            P("rep", "shard"),
            P("shard", None),
            P("shard", None),
            P("shard", None),
            P("shard", None),
            P(),
            P(),
            P(),
            P(),
            P(),
            P(),
            P(),
            P(),
        ),
        out_specs=(
            P("rep", "shard", None),
            P("rep", "shard", None, None),
            P("rep", "shard", None),
            P("rep", "shard", None),
            P("rep", "shard", None, None),
            P("shard", None),
            P("shard", None),
            P("shard", None),
            P("shard", None),
            P(),
            P(),
            P(),
            P(),
            P(),
            P(),
            P(),
            P(),
        ),
        check_vma=False,
    )
```

profile of v0, /device:TPU:1, one launch (start us, length us, event | category | flops | bytes accessed | tf_op | source)
XLA Modules:
  0.0 1008.6 jit_solution(7969806802003201834)
XLA Ops:
  7.3 2.6 convert_element_type.145
  10.5 33.0 %all-gather.7.cloned.1.call-done = bf16[768,2304]{1,0:T(8,128)(2,1)} async-done(((bf16[192,2304]{1,0:T(8,128)(2,1)}), bf16[768,2304]{1,0:T(8,128)(2,1)}) %all-gather.7.cloned.1.call-update) | async-done | bytes 3538960 | tf_op jit(solution)/shard_map/all_gather | solution.py:138
  43.5 5.3 add_convert_fusion.1
  54.5 2.9 convert_element_type.154
  60.2 2.6 fusion.99
  65.2 6.2 all-gather.11.cloned.1.call-done
  73.2 20.0 %all-gather.9.cloned.1.call-done = bf16[1024,768]{1,0:T(8,128)(2,1)} async-done(((bf16[256,768]{1,0:T(8,128)(2,1)}), bf16[1024,768]{1,0:T(8,128)(2,1)}) %all-gather.9.cloned.1.call-update) | async-done | bytes 1572880 | tf_op jit(solution)/shard_map/all_gather | solution.py:152
  93.2 3.2 pad_maximum_fusion.2
  97.5 133.8 %while.28 = (s32[]{:T(128)}, bf16[12,768,64]{1,2,0:T(8,128)(2,1)}, f32[12,768]{1,0:T(8,128)}, s32[12]{0:T(128)S(1)}, bf16[768,768]{1,0:T(8,128)(2,1)}, /*index=5...) while((s32[]{:T(128)}, bf16[12,768,64]{1,2,0:T(8,128)(2,1)}, ...), condition=%wide.region_3.4_spmd.clone, body=%wide.region_0.3_spmd.clone.sunk | while | flops 312605952 | bytes 34253524 | solution.py:64
  104.5 4.1 fusion.160
  115.6 4.1 fusion.160
  126.8 4.1 fusion.160
  137.9 4.1 fusion.160
  149.0 4.1 fusion.160
  160.1 4.6 fusion.160
  171.7 4.1 fusion.160
  182.8 4.2 fusion.160
  193.9 4.1 fusion.160
  205.0 4.1 fusion.160
  216.1 4.1 fusion.160
  227.2 4.1 fusion.160
  232.8 3.1 fusion.100
  236.7 29.4 %multiply_convert_fusion.1 = (bf16[768,3072]{1,0:T(8,128)(2,1)}, f32[768,3072]{1,0:T(8,128)}, f32[768,3072]{1,0:T(8,128)}) fusion(f32[3072]{0:T(1024)S(1)} %copy-done.42, bf16[768,3072]{1,0:T(8,128)(2,1)} %all-gather.15.cloned.1.call-done, f32[768,768]{0,1:T(8,128)S(1)} %get-tuple-element.319, f32[768]{0:T(1024)S(1)} %get-tuple-element.226, ...), kind=kOutput, calls=%fused_computation.48 | convolution fusion | flops 3782541312 | bytes 30695424 | tf_op jit(solution)/shard_map/dot_general | solution.py:16
  266.1 8.7 fusion.101
  294.3 13.0 %convert_reduce_fusion = (f32[3072]{0:T(1024)S(1)}, bf16[768,3072]{1,0:T(8,128)(2,1)S(1)}) fusion(f32[768,3072]{1,0:T(8,128)} %get-tuple-element.302, f32[768,3072]{1,0:T(8,128)} %get-tuple-element.320, f32[3072]{0:T(1024)S(1)} %copy-done.43, bf16[768,768]{0,1:T(8,128)(2,1)S(1)} %get-tuple-element.288, bf16[3072,768]{1,0:T(8,128)(2,1)} %all-gather.17.cloned.1.call-done), kind=kOutput, calls=%fused_computation.46 | convolution fusion | flops 3663983616 | bytes 29515776 | tf_op jit(solution)/shard_map/dot_general | solution.py:26
  307.3 4.5 multiply_reduce_fusion.2
  317.2 168.6 %while.29 = (s32[]{:T(128)}, bf16[12,768,64]{1,2,0:T(8,128)(2,1)}, bf16[12,1536,64]{1,2,0:T(8,128)(2,1)}, bf16[12,1536,64]{1,2,0:T(8,128)(2,1)}, s32[12]{0:T(128...) while((s32[]{:T(128)}, bf16[12,768,64]{1,2,0:T(8,128)(2,1)}, ...), condition=%wide.region_23.24_spmd.clone, body=%wide.region_21.23_spmd.clone.sunk | while | flops 766917888 | bytes 38360792 | solution.py:86
  319.2 2.5 subtract_exponential_fusion.6
  326.5 2.5 fusion.169
  333.3 2.5 subtract_exponential_fusion.6
  340.5 2.5 fusion.169
  347.3 2.5 subtract_exponential_fusion.6
  354.6 2.5 fusion.169
  361.3 2.5 subtract_exponential_fusion.6
  368.6 2.5 fusion.169
  375.4 2.5 subtract_exponential_fusion.6
  382.7 2.5 fusion.169
  389.4 2.5 subtract_exponential_fusion.6
  396.7 2.5 fusion.169
  403.5 2.5 subtract_exponential_fusion.6
  410.8 2.5 fusion.169
  417.6 2.5 subtract_exponential_fusion.6
  424.8 2.5 fusion.169
  431.6 2.5 subtract_exponential_fusion.6
  438.9 2.5 fusion.169
  445.7 2.5 subtract_exponential_fusion.6
  453.0 2.5 fusion.169
  459.7 2.5 subtract_exponential_fusion.6
  467.0 2.5 fusion.169
  481.1 2.5 fusion.169
  496.9 32.2 %reduce-scatter.8.cloned.1.call-done = bf16[256,1536]{0,1:T(8,128)(2,1)} async-done(((bf16[1024,1536]{0,1:T(8,128)(2,1)}), bf16[256,1536]{0,1:T(8,128)(2,1)}) %reduce-scatter.8.cloned.1.call-update) | async-done | bytes 786448 | tf_op jit(solution)/shard_map/reduce_scatter | solution.py:243
  534.6 5.8 copy.89
  540.5 3.8 convolution_convert_fusion.2
  544.3 9.7 convolution_convert_fusion.1
  554.1 8.7 convolution_convert_fusion
  562.9 18.1 %reduce-scatter.16.cloned.1.call-done = bf16[192,2304]{1,0:T(8,128)(2,1)} async-done(((bf16[768,2304]{1,0:T(8,128)(2,1)}), bf16[192,2304]{1,0:T(8,128)(2,1)}) %reduce-scatter.16.cloned.1.call-update) | async-done | bytes 884752
  583.3 26.6 %reduce-scatter.10.cloned.1.call-done = bf16[192,768]{1,0:T(8,128)(2,1)} async-done(((bf16[768,768]{1,0:T(8,128)(2,1)}), bf16[192,768]{1,0:T(8,128)(2,1)}) %reduce-scatter.10.cloned.1.call-update) | async-done | bytes 294928 | tf_op jit(solution)/shard_map/reduce_scatter | solution.py:271
  609.9 50.4 %reduce-scatter.12.cloned.1.call-done = bf16[192,3072]{1,0:T(8,128)(2,1)} async-done(((bf16[768,3072]{1,0:T(8,128)(2,1)}), bf16[192,3072]{1,0:T(8,128)(2,1)}) %reduce-scatter.12.cloned.1.call-update) | async-done | bytes 1179664 | tf_op jit(solution)/shard_map/reduce_scatter | solution.py:274
  660.3 50.4 %reduce-scatter.14.cloned.1.call-done = bf16[768,768]{1,0:T(8,128)(2,1)} async-done(((bf16[3072,768]{1,0:T(8,128)(2,1)}), bf16[768,768]{1,0:T(8,128)(2,1)}) %reduce-scatter.14.cloned.1.call-update) | async-done | bytes 1179664 | tf_op jit(solution)/shard_map/reduce_scatter | solution.py:277
  724.7 3.4 fusion.47
  736.4 43.8 %all-reduce.1 = (f32[6,768]{1,0:T(8,128)}, f32[2,768]{1,0:T(2,128)}, f32[3072]{0:T(1024)}, f32[3,128]{1,0:T(4,128)}, f32[128,14]{0,1:T(8,128)}, /*index=5*/f32[14]{0:T(128)}) all-reduce(f32[6,768]{1,0:T(8,128)S(1)} %stack.32, f32[2,768]{1,0:T(2,128)S(1)} %pad_maximum_fusion.11, ...), channel_id=1, replica_groups=mesh['rep'=8,'shard'=4] {'rep','shard'}, use_global_device_ids=true, to_apply=%region_40.41 | all-reduce | flops 11406 | bytes 91248 | tf_op jit(solution)/shard_map/psum | solution.py:292
  780.2 85.0 %all-reduce.9.cloned.1.call-done = (bf16[192,2304]{0,1:T(8,128)(2,1)}, bf16[192,768]{1,0:T(8,128)(2,1)}, bf16[192,3072]{1,0:T(8,128)(2,1)}, bf16[768,768]{1,0:T(8,128)(2,1)}) async-done(((bf16[192,2304]{0,1:T(8,128)(2,1)}, bf16[192,768]{1,0:T(8,128)(2,1)}, bf16[192,3072]{1,0:T(8,128)(2,1)}, bf16[768,768]{1,0:T(8,128)(2,1)}), (bf16[192,2304]{0,1:T(8,128)(2,1)}, bf16[192,768]{1,0:T(8,128)(2,1)}, ...) | async-done | bytes 3538960 | tf_op jit(solution)/shard_map/psum | solution.py:282
  865.2 3.0 convert_element_type.173
  872.3 126.1 %all-reduce.7.cloned.1.call-done = (f32[768,128]{1,0:T(8,128)}, f32[128,128]{1,0:T(8,128)}) async-done(((f32[768,128]{1,0:T(8,128)}, f32[128,128]{1,0:T(8,128)}), (f32[768,128]{1,0:T(8,128)}, f32[128,128]{1,0:T(8,128)})) %all-reduce.7.cloned.1.call-update) | async-done | bytes 458768 | tf_op jit(solution)/shard_map/psum | solution.py:292
  (407 shorter events, 265.4 us)
Async XLA Ops:
  7.2 271.8 %copy-start = (f32[128,128]{1,0:T(8,128)S(1)}, f32[128,128]{1,0:T(8,128)}, u32[]{:S(2)}) copy-start(f32[128,128]{1,0:T(8,128)} %param.35) | copy-start | bytes 196612
  7.2 2.7 copy-start.13
  7.2 3.0 copy-start.17
  7.2 3.2 copy-start.36
  7.2 36.3 %all-gather.7.cloned.1.call-start = ((), (), s32[]{:S(2)}) async-start(), calls=%async_computation.5 | async-start | bytes 4423680 | tf_op jit(solution)/shard_map/all_gather | solution.py:138
  9.9 61.5 %all-gather.11.cloned.1.call-start = ((), (), s32[]{:S(2)}) async-start(), calls=%async_computation.7 | async-start | bytes 1966080 | tf_op jit(solution)/shard_map/all_gather | solution.py:153
  10.2 33.3 %copy-start.27 = (bf16[1,1,512,768]{2,3,1,0:T(8,128)(2,1)}, bf16[1,1,512,768]{2,3,1,0:T(8,128)(2,1)S(1)}, u32[]{:S(2)}) copy-start(bf16[1,1,512,768]{2,3,1,0:T(8,128)(2,1)S(1)} %copy.63) | copy-start | bytes 2359300
  10.4 33.1 %copy-start.31 = (bf16[1,256,768]{1,2,0:T(8,128)(2,1)}, bf16[1,256,768]{1,2,0:T(8,128)(2,1)S(1)}, u32[]{:S(2)}) copy-start(bf16[1,256,768]{1,2,0:T(8,128)(2,1)S(1)} %copy.62) | copy-start | bytes 1179652
  43.5 8.8 copy-start.29
  48.9 1.8 copy-start.12
  50.6 2.6 copy-start.16
  51.6 41.6 %all-gather.9.cloned.1.call-start = ((), (), s32[]{:S(2)}) async-start(), calls=%async_computation.6 | async-start | bytes 1966080 | tf_op jit(solution)/shard_map/all_gather | solution.py:152
  52.3 179.1 %all-gather.13.cloned.1.call-start = ((), (), s32[]{:S(2)}) async-start(), calls=%async_computation.8 | async-start | bytes 1474560 | tf_op jit(solution)/shard_map/all_gather | solution.py:139
  53.1 183.2 %all-gather.15.cloned.1.call-start = ((), (), s32[]{:S(2)}) async-start(), calls=%async_computation.9 | async-start | bytes 5898240 | tf_op jit(solution)/shard_map/all_gather | solution.py:140
  54.4 3.1 copy-start.37
  54.4 3.1 copy-start.38
  54.4 4.5 copy-start.26
  54.4 4.8 copy-start.30
  54.4 211.7 %all-gather.17.cloned.1.call-start = ((), (), s32[]{:S(2)}) async-start(), calls=%async_computation.10 | async-start | bytes 5898240 | tf_op jit(solution)/shard_map/all_gather | solution.py:141
  57.4 471.7 %reduce-scatter.8.cloned.1.call-start = ((), (), s32[]{:S(2)}) async-start(), calls=%async_computation.11 | async-start | bytes 3932160 | tf_op jit(solution)/shard_map/reduce_scatter | solution.py:243
  101.0 2.1 copy-start.2
  112.1 2.1 copy-start.2
  123.3 2.2 copy-start.2
  134.4 2.1 copy-start.2
  145.5 2.1 copy-start.2
  156.6 2.1 copy-start.2
  168.2 2.1 copy-start.2
  179.3 2.1 copy-start.2
  190.4 2.1 copy-start.2
  201.5 2.1 copy-start.2
  212.6 2.1 copy-start.2
  223.7 2.1 copy-start.2
  231.4 1.4 copy-start.9
  235.9 30.1 %copy-start.6 = (f32[768,768]{0,1:T(8,128)}, f32[768,768]{0,1:T(8,128)S(1)}, u32[]{:S(2)}) copy-start(f32[768,768]{0,1:T(8,128)S(1)} %get-tuple-element.319) | copy-start | bytes 7077892
  275.1 1.4 copy-start.18
  275.1 4.0 copy-start.35
  280.6 4.5 copy-start.39
  287.5 4.3 copy-start.11
  290.4 2.5 copy-start.23
  293.6 13.7 %slice-start = ((s8[4718592]{0:T(1024)(128)(4,1)}), s8[4194304]{0:T(1024)(128)(4,1)S(1)}, s32[]{:S(2)}) async-start(s8[4718592]{0:T(1024)(128)(4,1)} %bitcast.224), calls=%async_computation.18 | async-start | bytes 8388608
  293.9 13.4 %copy-start.19 = (bf16[768,768]{0,1:T(8,128)(2,1)}, bf16[768,768]{0,1:T(8,128)(2,1)S(1)}, u32[]{:S(2)}) copy-start(bf16[768,768]{0,1:T(8,128)(2,1)S(1)} %get-tuple-element.288) | copy-start | bytes 3538948
  294.3 13.0 %copy-start.7 = (f32[768,768]{0,1:T(8,128)S(1)}, f32[768,768]{0,1:T(8,128)}, u32[]{:S(2)}) copy-start(f32[768,768]{0,1:T(8,128)} %copy-done.6) | copy-start | bytes 7077892
  294.3 13.1 %slice-start.1 = ((s8[4718592]{0:T(1024)(128)(4,1)}), s8[524288]{0:T(1024)(128)(4,1)S(1)}, s32[]{:S(2)}) async-start(s8[4718592]{0:T(1024)(128)(4,1)} %bitcast.224), calls=%async_computation.19 | async-start | bytes 1048576
  307.3 4.6 copy-start.44
  312.8 3.3 copy-start.20
  491.0 90.0 %reduce-scatter.16.cloned.1.call-start = ((), (), s32[]{:S(2)}) async-start(), calls=%async_computation.15 | async-start | bytes 4423680
  491.3 3.5 copy-start.4
  491.3 3.5 copy-start.28
  491.3 3.4 copy-start.32
  529.0 2.1 copy-start.14
  529.0 2.1 copy-start.15
  531.2 1.4 copy-start.22
  540.4 69.5 %reduce-scatter.10.cloned.1.call-start = ((), (), s32[]{:S(2)}) async-start(), calls=%async_computation.12 | async-start | bytes 1474560 | tf_op jit(solution)/shard_map/reduce_scatter | solution.py:271
  544.2 116.1 %reduce-scatter.12.cloned.1.call-start = ((), (), s32[]{:S(2)}) async-start(), calls=%async_computation.13 | async-start | bytes 5898240 | tf_op jit(solution)/shard_map/reduce_scatter | solution.py:274
  554.1 156.7 %reduce-scatter.14.cloned.1.call-start = ((), (), s32[]{:S(2)}) async-start(), calls=%async_computation.14 | async-start | bytes 5898240 | tf_op jit(solution)/shard_map/reduce_scatter | solution.py:277
  562.9 302.3 %all-reduce.9.cloned.1.call-start = ((), (), s32[]{:S(2)}) async-start(), calls=%async_computation.17 | async-start | bytes 7667712 | tf_op jit(solution)/shard_map/psum | solution.py:282
  710.8 287.6 %all-reduce.7.cloned.1.call-start = ((), (), s32[]{:S(2)}) async-start(), calls=%async_computation.16 | async-start | bytes 917504 | tf_op jit(solution)/shard_map/psum | solution.py:292
  715.4 7.0 copy-start.24
  724.7 3.4 copy-start.10
  724.7 3.6 copy-start.33
  865.2 3.0 copy-start.21
  868.2 1.7 copy-start.25
  869.8 1.6 copy-start.34
  869.8 131.9 %copy-start.1 = (f32[128,128]{1,0:T(8,128)S(1)}, f32[128,128]{1,0:T(8,128)}, u32[]{:S(2)}) copy-start(f32[128,128]{1,0:T(8,128)} %param.35) | copy-start | bytes 196612
  (7 other events, 7.1 us)
Sparse Core Ops, SparseCore 0:
  10.2 33.2 all-gather.6
  51.7 19.6 all-gather.10
  73.5 19.6 all-gather.8
  95.2 17.4 all-gather.12
  114.7 37.4 all-gather.14
  153.6 37.4 all-gather.16
  491.1 37.8 reduce-scatter.7
  540.5 40.4 reduce-scatter.15
  584.1 25.7 reduce-scatter.9
  612.5 47.8 reduce-scatter.11
  662.9 47.8 reduce-scatter.13
  715.7 149.3 all-reduce.8
  872.0 126.3 all-reduce.6
where the time goes:
time: 1020 us; the launch traced here: 1010 us
  waiting for transfers between devices  449 us (44%)
  matrix products  322 us (32%)
  local copies, waits for them, and re-layouts  108 us (11%)
  other arithmetic  50.7 us (5%)
  blocking collectives  43.8 us (4%)
  between operations  17.9 us (2%)
  loops' own time  16.2 us (2%)
    dot_general x29, matrix products, dot_plain(): return jnp.dot(left, right, preferred_element_type=jnp.float32)  127 us
    psum x1, waiting for transfers between devices, body(): lax.psum((g_biases, g_gains, g_in_bias, g_student, g_vectors, g_pool, g_c...  126 us
    dot_general x42, matrix products, dot_second(): lax.dot_general(left, right, (((1,), (1,)), ((), ())), preferred_element_...  107 us
    psum x1, waiting for transfers between devices, body(): lax.psum(owned[0].astype(jnp.bfloat16), 'rep').astype(jnp.float32)  85 us
    dot_general x30, matrix products, dot_first(): lax.dot_general(left, right, (((0,), (0,)), ((), ())), preferred_element_...  82.1 us
    reduce_scatter x1, waiting for transfers between devices, body(): lax.psum_scatter(g_ffo.astype(jnp.bfloat16), 'shard', scatter_dimension=0...  50.4 us
    reduce_scatter x1, waiting for transfers between devices, body(): lax.psum_scatter(g_in.astype(jnp.bfloat16), 'shard', scatter_dimension=0,...  50.4 us
    psum x1, blocking collectives, body(): lax.psum((g_biases, g_gains, g_in_bias, g_student, g_vectors, g_pool, g_c...  43.8 us
  transfers between devices with their start and end apart: 13, of which 10 were waited for; matrix products, arithmetic and copies ran while one was open for 22% of the time, Pallas kernels for 0%

commit v1 on v0

--- a/solution.py
+++ b/solution.py
@@ -10,6 +10,24 @@
 SHEADS = 2
 HIGHEST = lax.Precision.HIGHEST
 NEG_BIG = -1e30
+
+
+def collect(array, axis, dim):
+    ways, here, hop = (lax.axis_size(axis), lax.axis_index(axis), array.shape[dim])
+    lengths = [n * ways if d == dim else n for d, n in enumerate(array.shape)]
+    full = lax.dynamic_update_slice_in_dim(
+        jnp.zeros(lengths, array.dtype), array, here * hop, axis=dim
+    )
+    going_up = going_down = array
+    for far in range(1, ways // 2 + 1):
+        going_up = lax.ppermute(going_up, axis, [(d, (d + 1) % ways) for d in range(ways)])
+        full = lax.dynamic_update_slice_in_dim(full, going_up, (here - far) % ways * hop, axis=dim)
+        if 2 * far < ways:
+            going_down = lax.ppermute(going_down, axis, [(d, (d - 1) % ways) for d in range(ways)])
+            full = lax.dynamic_update_slice_in_dim(
+                full, going_down, (here + far) % ways * hop, axis=dim
+            )
+    return full
 
 
 def dot_plain(left, right):
@@ -135,7 +153,7 @@
     in_low = w_in.astype(jnp.bfloat16)
     ffo_low = w_ffo.astype(jnp.bfloat16)
     qkv_full, out_full, in_full, ffo_full = (
-        lax.all_gather(qkv_low, "shard", axis=0, tiled=True),
+        collect(qkv_low, "shard", 0),
         lax.all_gather(out_low, "shard", axis=0, tiled=True),
         lax.all_gather(in_low, "shard", axis=0, tiled=True),
         lax.all_gather(ffo_low, "shard", axis=0, tiled=True),

time: 1020 us -> 1060 us (1.039)
  waiting for transfers between devices: 449 us -> 470 us
    ppermute x0 -> x3, waiting for transfers between devices: none -> 22.5 us  [the longest x2 22.5 us: collect(): lax.ppermute(going_up, axis, [(d, (d + 1) % ways) for d in range(ways)])]
    all_gather x1, waiting for transfers between devices: 33 us -> 18.9 us  [body(): lax.all_gather(qkv_low, 'shard', axis=0, tiled=True)]
    psum x1, waiting for transfers between devices: 85 us -> 96.4 us  [body(): lax.psum(owned[0].astype(jnp.bfloat16), 'rep').astype(jnp.float32)]
    unnamed x105 -> x109, local copies, waits for them, and re-layouts: 30.3 us -> 33 us
  transfers between devices with their start and end apart: 13 -> 16, of which waited for: 10 -> 12; matrix products, arithmetic and copies ran while one was open for 22% -> 22% of each run, Pallas kernels for 0% -> 0%
where the time goes in v1:
time: 1060 us; the launch traced here: 1040 us
  waiting for transfers between devices  470 us (44%)
  matrix products  322 us (30%)
  local copies, waits for them, and re-layouts  118 us (11%)
  other arithmetic  49.2 us (5%)
  blocking collectives  45.4 us (4%)
  between operations  17.8 us (2%)
  loops' own time  16.2 us (2%)
    dot_general x29, matrix products, dot_plain(): return jnp.dot(left, right, preferred_element_type=jnp.float32)  127 us
    psum x1, waiting for transfers between devices, body(): lax.psum((g_biases, g_gains, g_in_bias, g_student, g_vectors, g_pool, g_c...  126 us
    dot_general x42, matrix products, dot_second(): lax.dot_general(left, right, (((1,), (1,)), ((), ())), preferred_element_...  107 us
    psum x1, waiting for transfers between devices, body(): lax.psum(owned[0].astype(jnp.bfloat16), 'rep').astype(jnp.float32)  96.4 us
    dot_general x30, matrix products, dot_first(): lax.dot_general(left, right, (((0,), (0,)), ((), ())), preferred_element_...  82.2 us
    reduce_scatter x1, waiting for transfers between devices, body(): lax.psum_scatter(g_ffo.astype(jnp.bfloat16), 'shard', scatter_dimension=0...  50.6 us
    reduce_scatter x1, waiting for transfers between devices, body(): lax.psum_scatter(g_in.astype(jnp.bfloat16), 'shard', scatter_dimension=0,...  50.3 us
    psum x1, blocking collectives, body(): lax.psum((g_biases, g_gains, g_in_bias, g_student, g_vectors, g_pool, g_c...  45.4 us
  transfers between devices with their start and end apart: 16, of which 12 were waited for; matrix products, arithmetic and copies ran while one was open for 22% of the time, Pallas kernels for 0%

profile of v1, /device:TPU:1, one launch (start us, length us, event | category | flops | bytes accessed | tf_op | source)
XLA Modules:
  0.0 1044.4 jit_solution(5081713423551176880)
XLA Ops:
  10.4 2.6 collective-permute-start
  13.0 19.4 %collective-permute-done = bf16[192,2304]{1,0:T(8,128)(2,1)S(1)} collective-permute-done((bf16[192,2304]{1,0:T(8,128)(2,1)S(1)}, bf16[192,2304]{1,0:T(8,128)(2,1)S(1)}, u32[]{:S(2)}, u32[]{:S(2)}) %collective-permute-start) | collective-permute-done | bytes 884768 | tf_op jit(solution)/shard_map/ppermute | solution.py:23
  41.8 3.1 collective-permute-done.2
  45.9 5.3 add_convert_fusion.1
  56.9 2.9 convert_element_type.154
  62.6 2.9 fusion.99
  67.9 7.5 all-gather.9.cloned.1.call-done
  77.2 20.0 %all-gather.7.cloned.1.call-done = bf16[1024,768]{1,0:T(8,128)(2,1)} async-done(((bf16[256,768]{1,0:T(8,128)(2,1)}), bf16[1024,768]{1,0:T(8,128)(2,1)}) %all-gather.7.cloned.1.call-update) | async-done | bytes 1572880 | tf_op jit(solution)/shard_map/all_gather | solution.py:170
  97.2 3.2 pad_maximum_fusion.2
  101.5 133.9 %while.28 = (s32[]{:T(128)}, bf16[12,768,64]{1,2,0:T(8,128)(2,1)}, f32[12,768]{1,0:T(8,128)}, s32[12]{0:T(128)S(1)}, bf16[768,768]{1,0:T(8,128)(2,1)}, /*index=5...) while((s32[]{:T(128)}, bf16[12,768,64]{1,2,0:T(8,128)(2,1)}, ...), condition=%wide.region_3.4_spmd.clone, body=%wide.region_0.3_spmd.clone.sunk | while | flops 312605952 | bytes 34253524 | solution.py:82
  108.5 4.1 fusion.160
  119.6 4.1 fusion.160
  130.9 4.1 fusion.160
  142.0 4.2 fusion.160
  153.1 4.1 fusion.160
  164.2 4.6 fusion.160
  175.8 4.1 fusion.160
  186.9 4.2 fusion.160
  198.0 4.1 fusion.160
  209.1 4.1 fusion.160
  220.2 4.1 fusion.160
  231.3 4.1 fusion.160
  236.8 3.1 fusion.100
  240.7 29.4 %multiply_convert_fusion.1 = (bf16[768,3072]{1,0:T(8,128)(2,1)}, f32[768,3072]{1,0:T(8,128)}, f32[768,3072]{1,0:T(8,128)}) fusion(f32[3072]{0:T(1024)S(1)} %copy-done.44, bf16[768,3072]{1,0:T(8,128)(2,1)} %all-gather.13.cloned.1.call-done, f32[768,768]{0,1:T(8,128)S(1)} %get-tuple-element.321, f32[768]{0:T(1024)S(1)} %get-tuple-element.226, ...), kind=kOutput, calls=%fused_computation.48 | convolution fusion | flops 3782541312 | bytes 30695424 | tf_op jit(solution)/shard_map/dot_general | solution.py:34
  270.1 8.7 fusion.101
  298.3 13.0 %convert_reduce_fusion = (f32[3072]{0:T(1024)S(1)}, bf16[768,3072]{1,0:T(8,128)(2,1)S(1)}) fusion(f32[768,3072]{1,0:T(8,128)} %get-tuple-element.302, f32[768,3072]{1,0:T(8,128)} %get-tuple-element.322, f32[3072]{0:T(1024)S(1)} %copy-done.45, bf16[768,768]{0,1:T(8,128)(2,1)S(1)} %get-tuple-element.288, bf16[3072,768]{1,0:T(8,128)(2,1)} %all-gather.15.cloned.1.call-done), kind=kOutput, calls=%fused_computation.46 | convolution fusion | flops 3663983616 | bytes 29515776 | tf_op jit(solution)/shard_map/dot_general | solution.py:44
  311.4 4.5 multiply_reduce_fusion.2
  321.3 168.7 %while.29 = (s32[]{:T(128)}, bf16[12,768,64]{1,2,0:T(8,128)(2,1)}, bf16[12,1536,64]{1,2,0:T(8,128)(2,1)}, bf16[12,1536,64]{1,2,0:T(8,128)(2,1)}, s32[12]{0:T(128...) while((s32[]{:T(128)}, bf16[12,768,64]{1,2,0:T(8,128)(2,1)}, ...), condition=%wide.region_23.24_spmd.clone, body=%wide.region_21.23_spmd.clone.sunk | while | flops 766917888 | bytes 38360792 | solution.py:104
  323.3 2.5 subtract_exponential_fusion.6
  330.6 2.5 fusion.169
  337.4 2.5 subtract_exponential_fusion.6
  344.6 2.5 fusion.169
  351.4 2.5 subtract_exponential_fusion.6
  358.7 2.5 fusion.169
  365.4 2.5 subtract_exponential_fusion.6
  372.7 2.5 fusion.169
  379.5 2.5 subtract_exponential_fusion.6
  386.8 2.5 fusion.169
  393.6 2.5 subtract_exponential_fusion.6
  400.9 2.5 fusion.169
  414.9 2.5 fusion.169
  421.7 2.5 subtract_exponential_fusion.6
  429.0 2.5 fusion.169
  443.0 2.5 fusion.169
  449.8 2.5 subtract_exponential_fusion.6
  457.1 2.5 fusion.169
  463.9 2.5 subtract_exponential_fusion.6
  471.1 2.5 fusion.169
  485.2 2.5 fusion.169
  501.0 32.0 %reduce-scatter.8.cloned.1.call-done = bf16[256,1536]{0,1:T(8,128)(2,1)} async-done(((bf16[1024,1536]{0,1:T(8,128)(2,1)}), bf16[256,1536]{0,1:T(8,128)(2,1)}) %reduce-scatter.8.cloned.1.call-update) | async-done | bytes 786448 | tf_op jit(solution)/shard_map/reduce_scatter | solution.py:261
  538.5 5.8 copy.89
  544.4 3.8 convolution_convert_fusion.2
  548.2 9.4 convolution_convert_fusion
  557.6 9.2 convolution_convert_fusion.1
  567.7 17.2 %reduce-scatter.16.cloned.1.call-done = bf16[192,2304]{1,0:T(8,128)(2,1)} async-done(((bf16[768,2304]{1,0:T(8,128)(2,1)}), bf16[192,2304]{1,0:T(8,128)(2,1)}) %reduce-scatter.16.cloned.1.call-update) | async-done | bytes 884752
  587.2 26.5 %reduce-scatter.10.cloned.1.call-done = bf16[192,768]{1,0:T(8,128)(2,1)} async-done(((bf16[768,768]{1,0:T(8,128)(2,1)}), bf16[192,768]{1,0:T(8,128)(2,1)}) %reduce-scatter.10.cloned.1.call-update) | async-done | bytes 294928 | tf_op jit(solution)/shard_map/reduce_scatter | solution.py:289
  613.8 50.6 %reduce-scatter.14.cloned.1.call-done = bf16[768,768]{1,0:T(8,128)(2,1)} async-done(((bf16[3072,768]{1,0:T(8,128)(2,1)}), bf16[768,768]{1,0:T(8,128)(2,1)}) %reduce-scatter.14.cloned.1.call-update) | async-done | bytes 1179664 | tf_op jit(solution)/shard_map/reduce_scatter | solution.py:295
  664.4 50.3 %reduce-scatter.12.cloned.1.call-done = bf16[192,3072]{1,0:T(8,128)(2,1)} async-done(((bf16[768,3072]{1,0:T(8,128)(2,1)}), bf16[192,3072]{1,0:T(8,128)(2,1)}) %reduce-scatter.12.cloned.1.call-update) | async-done | bytes 1179664 | tf_op jit(solution)/shard_map/reduce_scatter | solution.py:292
  728.6 18.9 %all-gather.17.cloned.1.call-done = bf16[768,2304]{1,0:T(8,128)(2,1)} async-done(((bf16[192,2304]{1,0:T(8,128)(2,1)}), bf16[768,2304]{1,0:T(8,128)(2,1)}) %all-gather.17.cloned.1.call-update) | async-done | bytes 3538960 | tf_op jit(solution)/shard_map/all_gather | solution.py:224
  747.5 3.4 fusion.47
  759.2 45.4 %all-reduce.1 = (f32[6,768]{1,0:T(8,128)}, f32[2,768]{1,0:T(2,128)}, f32[3072]{0:T(1024)}, f32[3,128]{1,0:T(4,128)}, f32[128,14]{0,1:T(8,128)}, /*index=5*/f32[14]{0:T(128)}) all-reduce(f32[6,768]{1,0:T(8,128)S(1)} %stack.32, f32[2,768]{1,0:T(2,128)S(1)} %pad_maximum_fusion.11, ...), channel_id=1, replica_groups=mesh['rep'=8,'shard'=4] {'rep','shard'}, use_global_device_ids=true, to_apply=%region_40.41 | all-reduce | flops 11406 | bytes 91248 | tf_op jit(solution)/shard_map/psum | solution.py:310
  804.6 96.4 %all-reduce.9.cloned.1.call-done = (bf16[192,2304]{0,1:T(8,128)(2,1)}, bf16[192,768]{1,0:T(8,128)(2,1)}, bf16[192,3072]{1,0:T(8,128)(2,1)}, bf16[768,768]{1,0:T(8,128)(2,1)}) async-done(((bf16[192,2304]{0,1:T(8,128)(2,1)}, bf16[192,768]{1,0:T(8,128)(2,1)}, bf16[192,3072]{1,0:T(8,128)(2,1)}, bf16[768,768]{1,0:T(8,128)(2,1)}), (bf16[192,2304]{0,1:T(8,128)(2,1)}, bf16[192,768]{1,0:T(8,128)(2,1)}, ...) | async-done | bytes 3538960 | tf_op jit(solution)/shard_map/psum | solution.py:300
  901.0 3.0 convert_element_type.173
  908.1 126.1 %all-reduce.7.cloned.1.call-done = (f32[768,128]{1,0:T(8,128)}, f32[128,128]{1,0:T(8,128)}) async-done(((f32[768,128]{1,0:T(8,128)}, f32[128,128]{1,0:T(8,128)}), (f32[768,128]{1,0:T(8,128)}, f32[128,128]{1,0:T(8,128)})) %all-reduce.7.cloned.1.call-update) | async-done | bytes 458768 | tf_op jit(solution)/shard_map/psum | solution.py:310
  (421 shorter events, 284.1 us)
Async XLA Ops:
  7.2 275.8 %copy-start = (f32[128,128]{1,0:T(8,128)S(1)}, f32[128,128]{1,0:T(8,128)}, u32[]{:S(2)}) copy-start(f32[128,128]{1,0:T(8,128)} %param.35) | copy-start | bytes 196612
  7.2 2.1 copy-start.18
  7.2 68.1 %all-gather.9.cloned.1.call-start = ((), (), s32[]{:S(2)}) async-start(), calls=%async_computation.6 | async-start | bytes 1966080 | tf_op jit(solution)/shard_map/all_gather | solution.py:171
  9.4 25.6 %copy-start.37 = (f32[6,768]{1,0:T(8,128)S(1)}, f32[6,768]{1,0:T(8,128)}, u32[]{:S(2)}) copy-start(f32[6,768]{1,0:T(8,128)} %param.30) | copy-start | bytes 55300
  9.4 26.2 %copy-start.14 = (bf16[1,1,512,768]{3,2,1,0:T(8,128)(2,1)S(1)}, bf16[1,1,512,768]{3,2,1,0:T(8,128)(2,1)}, u32[]{:S(2)}) copy-start(bf16[1,1,512,768]{3,2,1,0:T(8,128)(2,1)} %param.22) | copy-start | bytes 2359300
  10.4 31.4 %copy-start.13 = (bf16[192,2304]{1,0:T(8,128)(2,1)}, bf16[192,2304]{1,0:T(8,128)(2,1)S(1)}, u32[]{:S(2)}) copy-start(bf16[192,2304]{1,0:T(8,128)(2,1)S(1)} %get-tuple-element.304) | copy-start | bytes 2654212
  10.4 22.0 %collective-permute-start = (bf16[192,2304]{1,0:T(8,128)(2,1)S(1)}, bf16[192,2304]{1,0:T(8,128)(2,1)S(1)}, u32[]{:S(2)}, u32[]{:S(2)}) collective-permute-start(bf16[192,2304]{1,0:T(8,128)(2,1)S(1)} %get-tuple-element.304), channel_id=1, source_target_pairs={{0,1},{1,2},{2,3},{3,0},{4,5},{5,6},{6,7},{7,4},{8,9},{9,10},{10,1... | collective-permute-start | bytes 2654216 | tf_op jit(solution)/shard_map/ppermute | solution.py:23
  13.0 26.7 %collective-permute-start.1 = (bf16[192,2304]{1,0:T(8,128)(2,1)S(1)}, bf16[192,2304]{1,0:T(8,128)(2,1)}, u32[]{:S(2)}, u32[]{:S(2)}) collective-permute-start(bf16[192,2304]{1,0:T(8,128)(2,1)S(1)} %get-tuple-element.304), channel_id=1, source_target_pairs={{0,3},{1,0},{2,1},{3,2},{4,7},{5,4},{6,5},{7,6},{8,11},{9,8},{10,9... | collective-permute-start | bytes 2654216 | tf_op jit(solution)/shard_map/ppermute | solution.py:26
  32.4 12.5 %collective-permute-start.2 = (bf16[192,2304]{1,0:T(8,128)(2,1)S(1)}, bf16[192,2304]{1,0:T(8,128)(2,1)S(1)}, u32[]{:S(2)}, u32[]{:S(2)}) collective-permute-start(bf16[192,2304]{1,0:T(8,128)(2,1)S(1)} %collective-permute-done), channel_id=1, source_target_pairs={{0,1},{1,2},{2,3},{3,0},{4,5},{5,6},{6,7},{7,4},{8,9},{9,10},{10,1... | collective-permute-start | bytes 2654216 | tf_op jit(solution)/shard_map/ppermute | solution.py:23
  38.6 7.3 copy-start.28
  38.7 7.2 copy-start.32
  45.9 8.9 copy-start.30
  51.3 1.8 copy-start.12
  53.0 2.6 copy-start.17
  54.0 43.2 %all-gather.7.cloned.1.call-start = ((), (), s32[]{:S(2)}) async-start(), calls=%async_computation.5 | async-start | bytes 1966080 | tf_op jit(solution)/shard_map/all_gather | solution.py:170
  54.7 180.7 %all-gather.11.cloned.1.call-start = ((), (), s32[]{:S(2)}) async-start(), calls=%async_computation.7 | async-start | bytes 1474560 | tf_op jit(solution)/shard_map/all_gather | solution.py:157
  55.5 184.8 %all-gather.13.cloned.1.call-start = ((), (), s32[]{:S(2)}) async-start(), calls=%async_computation.8 | async-start | bytes 5898240 | tf_op jit(solution)/shard_map/all_gather | solution.py:158
  56.8 3.1 copy-start.38
  56.8 3.1 copy-start.39
  56.8 4.5 copy-start.27
  56.8 4.8 copy-start.31
  56.8 213.3 %all-gather.15.cloned.1.call-start = ((), (), s32[]{:S(2)}) async-start(), calls=%async_computation.9 | async-start | bytes 5898240 | tf_op jit(solution)/shard_map/all_gather | solution.py:159
  59.8 473.1 %reduce-scatter.8.cloned.1.call-start = ((), (), s32[]{:S(2)}) async-start(), calls=%async_computation.11 | async-start | bytes 3932160 | tf_op jit(solution)/shard_map/reduce_scatter | solution.py:261
  101.5 135.3 %copy-start.41 = (f32[768]{0:T(1024)S(1)}, f32[768]{0:T(1024)}, u32[]{:S(2)}) copy-start(f32[768]{0:T(1024)} %get-tuple-element.227) | copy-start | bytes 9220
  105.0 2.1 copy-start.2
  116.1 2.1 copy-start.2
  127.2 2.3 copy-start.2
  138.5 2.1 copy-start.2
  149.6 2.1 copy-start.2
  160.7 2.1 copy-start.2
  172.3 2.1 copy-start.2
  183.4 2.1 copy-start.2
  194.5 2.1 copy-start.2
  205.6 2.1 copy-start.2
  216.7 2.1 copy-start.2
  227.8 2.1 copy-start.2
  240.0 30.1 %copy-start.6 = (f32[768,768]{0,1:T(8,128)}, f32[768,768]{0,1:T(8,128)S(1)}, u32[]{:S(2)}) copy-start(f32[768,768]{0,1:T(8,128)S(1)} %get-tuple-element.321) | copy-start | bytes 7077892
  279.1 4.1 copy-start.36
  284.6 4.5 copy-start.40
  291.5 4.3 copy-start.11
  294.4 2.5 copy-start.24
  297.6 13.7 %slice-start = ((s8[4718592]{0:T(1024)(128)(4,1)}), s8[4194304]{0:T(1024)(128)(4,1)S(1)}, s32[]{:S(2)}) async-start(s8[4718592]{0:T(1024)(128)(4,1)} %bitcast.224), calls=%async_computation.18 | async-start | bytes 8388608
  297.9 13.4 %copy-start.20 = (bf16[768,768]{0,1:T(8,128)(2,1)}, bf16[768,768]{0,1:T(8,128)(2,1)S(1)}, u32[]{:S(2)}) copy-start(bf16[768,768]{0,1:T(8,128)(2,1)S(1)} %get-tuple-element.288) | copy-start | bytes 3538948
  298.3 13.1 %copy-start.7 = (f32[768,768]{0,1:T(8,128)S(1)}, f32[768,768]{0,1:T(8,128)}, u32[]{:S(2)}) copy-start(f32[768,768]{0,1:T(8,128)} %copy-done.6) | copy-start | bytes 7077892
  298.3 13.1 %slice-start.1 = ((s8[4718592]{0:T(1024)(128)(4,1)}), s8[524288]{0:T(1024)(128)(4,1)S(1)}, s32[]{:S(2)}) async-start(s8[4718592]{0:T(1024)(128)(4,1)} %bitcast.224), calls=%async_computation.19 | async-start | bytes 1048576
  311.3 4.6 copy-start.46
  316.9 3.2 copy-start.21
  495.1 89.8 %reduce-scatter.16.cloned.1.call-start = ((), (), s32[]{:S(2)}) async-start(), calls=%async_computation.15 | async-start | bytes 4423680
  495.4 3.5 copy-start.4
  495.4 3.5 copy-start.29
  495.4 3.5 copy-start.33
  533.0 2.1 copy-start.15
  533.0 2.1 copy-start.16
  544.3 69.4 %reduce-scatter.10.cloned.1.call-start = ((), (), s32[]{:S(2)}) async-start(), calls=%async_computation.12 | async-start | bytes 1474560 | tf_op jit(solution)/shard_map/reduce_scatter | solution.py:289
  548.2 116.2 %reduce-scatter.14.cloned.1.call-start = ((), (), s32[]{:S(2)}) async-start(), calls=%async_computation.14 | async-start | bytes 5898240 | tf_op jit(solution)/shard_map/reduce_scatter | solution.py:295
  557.6 157.1 %reduce-scatter.12.cloned.1.call-start = ((), (), s32[]{:S(2)}) async-start(), calls=%async_computation.13 | async-start | bytes 5898240 | tf_op jit(solution)/shard_map/reduce_scatter | solution.py:292
  566.9 180.6 %all-gather.17.cloned.1.call-start = ((), (), s32[]{:S(2)}) async-start(), calls=%async_computation.10 | async-start | bytes 4423680 | tf_op jit(solution)/shard_map/all_gather | solution.py:224
  567.6 333.4 %all-reduce.9.cloned.1.call-start = ((), (), s32[]{:S(2)}) async-start(), calls=%async_computation.17 | async-start | bytes 7667712 | tf_op jit(solution)/shard_map/psum | solution.py:300
  714.7 319.6 %all-reduce.7.cloned.1.call-start = ((), (), s32[]{:S(2)}) async-start(), calls=%async_computation.16 | async-start | bytes 917504 | tf_op jit(solution)/shard_map/psum | solution.py:310
  719.2 7.1 copy-start.25
  747.5 3.4 copy-start.10
  747.5 3.6 copy-start.34
  901.0 3.0 copy-start.22
  905.7 131.8 %copy-start.1 = (f32[128,128]{1,0:T(8,128)S(1)}, f32[128,128]{1,0:T(8,128)}, u32[]{:S(2)}) copy-start(f32[128,128]{1,0:T(8,128)} %param.35) | copy-start | bytes 196612
  (12 other events, 14.6 us)
Sparse Core Ops, SparseCore 0:
  54.1 21.2 all-gather.8
  77.5 19.6 all-gather.6
  99.3 17.4 all-gather.10
  118.8 37.4 all-gather.12
  157.7 37.4 all-gather.14
  495.2 37.6 reduce-scatter.7
  544.5 40.4 reduce-scatter.15
  588.1 25.6 reduce-scatter.9
  616.5 47.8 reduce-scatter.13
  666.7 47.8 reduce-scatter.11
  716.3 31.1 all-gather.16
  752.5 148.4 all-reduce.8
  907.8 126.3 all-reduce.6
